TPU v7x, 32 devices: a whole 2x2x4 slice. The times are simulated.
32 devices in a mesh: dp: 2 (over x), tp: 16 (over y, z, core).
Axes of the slice: x: 2, y: 2, z: 4, core: 2. Of those that a mesh axis runs over, the one named last changes fastest.
Arguments:
- x: bfloat16 [5120, 7168], P(('dp', 'tp')), parts along dimension 0
- w_gate: bfloat16 [7168, 18432], P(None, 'tp')
- w_up: bfloat16 [7168, 18432], P(None, 'tp')
- w_down: bfloat16 [18432, 7168], P('tp')
Outputs:
- output: bfloat16 [5120, 7168], P(('dp', 'tp')), parts along dimension 0
There are 2 independent parts. A program takes and returns all parts, laid end to end along the dimension named above; an argument that names none is the same for every part.
All inputs are finite; a program needn't handle non-finite values.
Results may differ from a plain program's by a relative error of at most 0.016.
Values are sent between devices in bfloat16 or wider.
A program may use at most 2 GiB of HBM per device.

v0:
```python
import jax
import jax.numpy as jnp
from jax import lax
from jax.sharding import PartitionSpec as P


def solution(mesh):
    def step(x, w_gate, w_up, w_down):
        rows = lax.all_gather(x, "tp", axis=0, tiled=True)
        gate = jnp.dot(rows, w_gate, preferred_element_type=jnp.float32)
        up = jnp.dot(rows, w_up, preferred_element_type=jnp.float32)
        hidden = (jax.nn.silu(gate) * up).astype(jnp.bfloat16)
        term = jnp.dot(hidden, w_down, preferred_element_type=jnp.float32).astype(jnp.bfloat16)
        return lax.psum_scatter(term, "tp", scatter_dimension=0, tiled=True)

    return jax.shard_map(
        step,
        mesh=mesh,
        in_specs=(P(("dp", "tp"), None), P(None, "tp"), P(None, "tp"), P("tp", None)),
        out_specs=P(("dp", "tp"), None),
        check_vma=False,
    )
```

profile of v0, /device:TPU:0, one launch (start us, length us, event | category | flops | bytes accessed | tf_op | source)
XLA Modules:
  0.0 723.8 jit_solution(13984175685544904121)
XLA Ops:
  6.5 0.0 all-gather.2.cloned.1.call-start
  6.5 0.7 all-gather.2.cloned.1.call-update
  7.3 0.0 reduce-scatter.2.cloned.1.call-start
  7.3 187.2 %all-gather.2.cloned.1.call-done = bf16[2560,7168]{1,0:T(8,128)(2,1)} async-done(((bf16[160,7168]{1,0:T(8,128)(2,1)}), bf16[2560,7168]{1,0:T(8,128)(2,1)}) %all-gather.2.cloned.1.call-update) | async-done | bytes 36700176 | tf_op jit(solution)/shard_map/all_gather | solution.py:9
  194.5 57.3 %fusion.1 = f32[2560,1152]{1,0:T(8,128)} fusion(bf16[2560,7168]{1,0:T(8,128)(2,1)} %all-gather.2.cloned.1.call-done, bf16[7168,1152]{1,0:T(8,128)(2,1)} %param.5), kind=kOutput, calls=%fused_computation.3 | convolution fusion | flops 42278584320 | bytes 65011712 | tf_op jit(solution)/shard_map/dot_general | solution.py:10
  251.7 56.8 %fusion = bf16[2560,1152]{1,0:T(8,128)(2,1)S(1)} fusion(bf16[2560,7168]{1,0:T(8,128)(2,1)} %all-gather.2.cloned.1.call-done, bf16[7168,1152]{1,0:T(8,128)(2,1)} %param.6, f32[2560,1152]{1,0:T(8,128)} %fusion.1), kind=kOutput, calls=%fused_computation.2 | convolution fusion | flops 42296279040 | bytes 70909952 | tf_op jit(solution)/shard_map/dot_general | solution.py:11
  308.5 54.6 %convolution_convert_fusion = bf16[2560,7168]{1,0:T(8,128)(2,1)} fusion(bf16[2560,1152]{1,0:T(8,128)(2,1)S(1)} %fusion, bf16[1152,7168]{1,0:T(8,128)(2,1)} %param.7), kind=kOutput, calls=%fused_computation | convolution fusion | flops 42296934400 | bytes 59113472 | tf_op jit(solution)/shard_map/dot_general | solution.py:13
  363.2 0.0 reduce-scatter.2.cloned.1.call-update
  363.2 353.8 %reduce-scatter.2.cloned.1.call-done = bf16[160,7168]{1,0:T(8,128)(2,1)} async-done(((bf16[2560,7168]{1,0:T(8,128)(2,1)}), bf16[160,7168]{1,0:T(8,128)(2,1)}) %reduce-scatter.2.cloned.1.call-update) | async-done | bytes 2293776 | tf_op jit(solution)/shard_map/reduce_scatter | solution.py:14
Async XLA Ops:
  6.5 187.9 %all-gather.2.cloned.1.call-start = ((), (), s32[]{:S(2)}) async-start(), calls=%async_computation.1 | async-start | bytes 38993920 | tf_op jit(solution)/shard_map/all_gather | solution.py:9
  7.3 709.7 %reduce-scatter.2.cloned.1.call-start = ((), (), s32[]{:S(2)}) async-start(), calls=%async_computation.2 | async-start | bytes 38993920 | tf_op jit(solution)/shard_map/reduce_scatter | solution.py:14
Sparse Core Ops, SparseCore 0:
  8.9 185.4 all-gather.1
  363.3 353.6 reduce-scatter.1
where the time goes:
time: 724 us
  waiting for transfers between devices  542 us (75%)
  matrix products  169 us (23%)
  between operations  13.4 us (2%)
    reduce_scatter x1, waiting for transfers between devices, step(): return lax.psum_scatter(term, 'tp', scatter_dimension=0, tiled=True)  354 us
    all_gather x1, waiting for transfers between devices, step(): rows = lax.all_gather(x, 'tp', axis=0, tiled=True)  187 us
    dot_general x1, matrix products, step(): gate = jnp.dot(rows, w_gate, preferred_element_type=jnp.float32)  57.3 us
    dot_general x1, matrix products, step(): up = jnp.dot(rows, w_up, preferred_element_type=jnp.float32)  56.8 us
    dot_general x1, matrix products, step(): jnp.dot(hidden, w_down, preferred_element_type=jnp.float32)  54.6 us
  transfers between devices with their start and end apart: 2, of which 2 were waited for; matrix products, arithmetic and copies ran while one was open for 0% of the time, Pallas kernels for 0%

commit v1 on v0

v1 whole, which is shorter than its diff:
```python
import functools

import jax
import jax.numpy as jnp
from jax import lax
from jax.experimental import pallas as pl
from jax.experimental.pallas import tpu as pltpu
from jax.sharding import PartitionSpec as P

RING = 8
F32 = jnp.float32
BF16 = jnp.bfloat16


def chip_at(p):
    return jnp.where(p < RING // 2, p, 3 * RING // 2 - 1 - p)


def kernel(
    x_ref, wg_ref, wu_ref, wd_ref,
    y_ref, xg, tg, sg,
    w1, w2, xbuf, fbuf, hbuf, sbuf,
    wsem, lsem, xsend, xrecv, psend, precv, tsend, trecv, ssend, srecv,
):
    n = RING
    rows, dim = x_ref.shape
    half = rows // 2
    ff = wg_ref.shape[1]

    me = lax.axis_index("tp")
    core = lax.rem(me, 2)
    pos = chip_at(me // 2)

    def device(p, c):
        return {"tp": chip_at(lax.rem(p + n, n)) * 2 + c}

    down = (device(pos + 1, core), device(pos - 1, core))
    partner = device(pos, 1 - core)

    def part(d):
        return pl.ds(d * half, half)

    def remote(src, dst, send, recv, to):
        return pltpu.make_async_remote_copy(
            src_ref=src, dst_ref=dst, send_sem=send, recv_sem=recv,
            device_id=to, device_id_type=pl.DeviceIdType.MESH,
        )

    def x_first(d):
        return remote(x_ref.at[part(d)], xg.at[1, 0, part(d)], xsend.at[0, d], xrecv.at[1, d], down[d])

    def x_on(s, d):
        return remote(xg.at[s, 0, part(d)], xg.at[s + 1, 0, part(d)], xsend.at[s, d], xrecv.at[s + 1, d], down[d])

    def x_side_own(d):
        return remote(x_ref.at[part(d)], xg.at[0, 1, part(d)], psend.at[0, d], precv.at[0, d], partner)

    def x_side(s, d):
        return remote(xg.at[s, 0, part(d)], xg.at[s, 1, part(d)], psend.at[s, d], precv.at[s, d], partner)

    def term_side(s):
        return remote(xbuf.at[pl.ds(0, rows)], tg.at[s], tsend.at[s], trecv.at[s], partner)

    def sum_on(s, d):
        return remote(sbuf.at[part(d)], sg.at[s + 1, part(d)], ssend.at[s, d], srecv.at[s + 1, d], down[d])

    def weights():
        return (
            pltpu.make_async_copy(wg_ref, w1.at[:, pl.ds(0, ff)], wsem.at[0]),
            pltpu.make_async_copy(wu_ref, w1.at[:, pl.ds(ff, ff)], wsem.at[1]),
            pltpu.make_async_copy(wd_ref, w2, wsem.at[2]),
        )

    barrier = pltpu.get_barrier_semaphore()
    for other in (*down, partner):
        pl.semaphore_signal(barrier, inc=1, device_id=other, device_id_type=pl.DeviceIdType.MESH)
    pl.semaphore_wait(barrier, 3)

    for d in range(2):
        x_first(d).start()
    for d in range(2):
        x_side_own(d).start()
    for copy in weights():
        copy.start()
    for copy in weights():
        copy.wait()

    n1 = 768
    n2 = 512
    wide = fbuf.shape[1]
    per = wide // n2
    low = pl.ds(0, rows)
    high = pl.ds(rows, rows)

    def step(s, carry):
        slot = lax.rem(s, n)

        @pl.when(s < n)
        def _():
            for d in range(2):
                x_on(s - 1, d).wait_recv()

        @pl.when(s < n - 1)
        def _():
            for d in range(2):
                x_on(s, d).start()

        @pl.when(s > 1)
        def _():
            term_side(s - 1).wait_send()

        own_copy = pltpu.make_async_copy(xg.at[slot, 0], xbuf.at[low], lsem.at[0])

        @pl.when(s < n)
        def _():
            for d in range(2):
                x_side(s, d).start()
            own_copy.start()

        @pl.when(s == n)
        def _():
            pltpu.make_async_copy(x_ref, xbuf.at[low], lsem.at[0]).start()

        for d in range(2):
            x_side(slot, d).wait_recv()
        side_copy = pltpu.make_async_copy(xg.at[slot, 1], xbuf.at[high], lsem.at[1])
        side_copy.start()
        own_copy.wait()
        side_copy.wait()

        def first(j, c):
            cols = pl.ds(pl.multiple_of(j * n1, n1), n1)
            fbuf[:, cols] = jnp.dot(xbuf[...], w1[:, cols], preferred_element_type=F32)
            return c

        lax.fori_loop(0, 2 * ff // n1, first, 0)

        def gated(j, c):
            at = pl.ds(pl.multiple_of(j * 32, 32), 32)
            gate = fbuf[at, pl.ds(0, ff)]
            up = fbuf[at, pl.ds(ff, ff)]
            hbuf[at, :] = (jax.nn.silu(gate) * up).astype(BF16)
            return c

        lax.fori_loop(0, 2 * rows // 32, gated, 0)

        def second(j, c):
            cols = pl.ds(pl.multiple_of(j * n2, n2), n2)
            term = jnp.dot(hbuf[...], w2[:, cols], preferred_element_type=F32)
            at = pl.ds(pl.multiple_of((j // per) * rows, rows), rows)
            fcols = pl.ds(pl.multiple_of(lax.rem(j, per) * n2, n2), n2)
            fbuf[at, fcols] = term[:rows]
            xbuf[low, cols] = term[rows:].astype(BF16)
            return c

        lax.fori_loop(0, dim // n2, second, 0)

        term_side(s).start()

        @pl.when(s == 1)
        def _():
            def clear(j, c):
                cols = pl.ds(pl.multiple_of(j * n2, n2), n2)
                sbuf[:, cols] = jnp.zeros((rows, n2), BF16)
                return c

            lax.fori_loop(0, dim // n2, clear, 0)

        term_side(s).wait_recv()
        term_copy = pltpu.make_async_copy(tg.at[s], xbuf.at[high], lsem.at[0])
        term_copy.start()

        def sum_copy(d):
            return pltpu.make_async_copy(sg.at[s, part(d)], sbuf.at[part(d)], lsem.at[2 + d])

        @pl.when(s > 1)
        def _():
            for d in range(2):
                sum_on(s - 1, d).wait_recv()
                sum_on(s - 1, d).wait_send()
                sum_copy(d).start()

        term_copy.wait()
        for d in range(2):
            @pl.when(s > 1)
            def _():
                sum_copy(d).wait()

            def add(j, c):
                cols = pl.ds(pl.multiple_of(j * n2, n2), n2)
                at = pl.ds(pl.multiple_of((j // per) * rows + d * half, half), half)
                fcols = pl.ds(pl.multiple_of(lax.rem(j, per) * n2, n2), n2)
                total = fbuf[at, fcols] + xbuf[pl.ds(rows + d * half, half), cols].astype(F32)
                sbuf[part(d), cols] = (total + sbuf[part(d), cols].astype(F32)).astype(BF16)
                return c

            lax.fori_loop(0, dim // n2, add, 0)

            @pl.when(s < n)
            def _():
                sum_on(s, d).start()

            @pl.when(s == n)
            def _():
                pltpu.make_async_copy(sbuf.at[part(d)], y_ref.at[part(d)], lsem.at[2 + d]).start()

        return carry

    lax.fori_loop(1, n + 1, step, 0)

    for d in range(2):
        pltpu.make_async_copy(sbuf.at[part(d)], y_ref.at[part(d)], lsem.at[2 + d]).wait()
    term_side(n).wait_send()
    for d in range(2):
        x_first(d).wait_send()
        x_side_own(d).wait_send()

    def drain(s, c):
        for d in range(2):
            x_side(s, d).wait_send()

            @pl.when(s < n - 1)
            def _():
                x_on(s, d).wait_send()
        return c

    lax.fori_loop(1, n, drain, 0)


def solution(mesh):
    assert mesh.shape["tp"] == 2 * RING

    def step(x, w_gate, w_up, w_down):
        rows, dim = x.shape
        ff = w_gate.shape[1]
        n = RING
        hbm = pl.BlockSpec(memory_space=pl.ANY)
        dma = pltpu.SemaphoreType.DMA
        outs = pl.pallas_call(
            kernel,
            out_shape=[
                jax.ShapeDtypeStruct((rows, dim), BF16),
                jax.ShapeDtypeStruct((n, 2, rows, dim), BF16),
                jax.ShapeDtypeStruct((n + 1, rows, dim), BF16),
                jax.ShapeDtypeStruct((n + 1, rows, dim), BF16),
            ],
            in_specs=[hbm] * 4,
            out_specs=[hbm] * 4,
            scratch_shapes=[
                pltpu.VMEM((dim, 2 * ff), BF16),
                pltpu.VMEM((ff, dim), BF16),
                pltpu.VMEM((2 * rows, dim), BF16),
                pltpu.VMEM((2 * rows, dim // 2), F32),
                pltpu.VMEM((2 * rows, ff), BF16),
                pltpu.VMEM((rows, dim), BF16),
                dma((3,)),
                dma((4,)),
                dma((n, 2)),
                dma((n, 2)),
                dma((n, 2)),
                dma((n, 2)),
                dma((n + 1,)),
                dma((n + 1,)),
                dma((n + 1, 2)),
                dma((n + 1, 2)),
            ],
            compiler_params=pltpu.CompilerParams(
                collective_id=0, has_side_effects=True, vmem_limit_bytes=67043328
            ),
        )(x, w_gate, w_up, w_down)
        return outs[0]

    return jax.shard_map(
        step,
        mesh=mesh,
        in_specs=(P(("dp", "tp"), None), P(None, "tp"), P(None, "tp"), P("tp", None)),
        out_specs=P(("dp", "tp"), None),
        check_vma=False,
    )
```

time: 724 us -> 379 us (0.52)
  waiting for transfers between devices: 542 us -> 0 us
  Pallas kernels: 0 us -> 373 us
  matrix products: 169 us -> 0 us
  between operations: 13.4 us -> 0.01 us
    pallas_call x0 -> x1, Pallas kernels: none -> 373 us  [step(): pl.pallas_call(kernel, out_shape=[jax.ShapeDtypeStruct((rows, dim), BF16)...]
    reduce_scatter x1 -> x0, waiting for transfers between devices: 354 us -> none  [step(): return lax.psum_scatter(term, 'tp', scatter_dimension=0, tiled=True)]
    all_gather x1 -> x0, waiting for transfers between devices: 187 us -> none  [step(): rows = lax.all_gather(x, 'tp', axis=0, tiled=True)]
    dot_general x3 -> x0, matrix products: 169 us -> none  [the longest x1 57.3 us: step(): gate = jnp.dot(rows, w_gate, preferred_element_type=jnp.float32)]
  transfers between devices with their start and end apart: 2 -> 0, of which waited for: 2 -> 0; matrix products, arithmetic and copies ran while one was open for 0% -> 0% of each run, Pallas kernels for 0% -> 0%
where the time goes in v1:
time: 379 us; the launch traced here: 376 us
  Pallas kernels  373 us (98%)
    pallas_call x1, Pallas kernels, step(): pl.pallas_call(kernel, out_shape=[jax.ShapeDtypeStruct((rows, dim), BF16)...  373 us

profile of v1, /device:TPU:0, one launch (start us, length us, event | category | flops | bytes accessed | tf_op | source)
XLA Modules:
  0.0 376.0 jit_solution(9346558310733076508)
XLA Ops:
  0.0 372.8 %shard_map.46 = (bf16[160,7168]{1,0:T(8,128)(2,1)}, bf16[8,2,160,7168]{3,2,1,0:T(8,128)(2,1)}, bf16[9,160,7168]{2,1,0:T(8,128)(2,1)}, bf16[9,160,7168]{2,1,0:T(8,128)(2,1)}) custom-call(bf16[160,7168]{1,0:T(8,128)(2,1)} %x_ref.1, bf16[7168,1152]{1,0:T(8,128)(2,1)} %wg_ref.1, bf16[7168,1152]{1,0:T(8,128)(2,1)} %wu_ref.1, bf16[1152,7168]{1,0:T(8,128)(2,1)} %wd_ref.1), custom_call_target="tpu_custom_call" | custom-call | tf_op jit(solution)/shard_map/pallas_call | solution.py:239
  372.8 3.2 copy.6

commit v2 on v0

v2 whole, which is shorter than its diff:
```python
import jax
import jax.numpy as jnp
from jax import lax
from jax.experimental import pallas as pl
from jax.experimental.pallas import tpu as pltpu
from jax.sharding import PartitionSpec as P

RING = 8
CHUNK = 16
K1 = 3584
N1 = 768
N2 = 1024
OWN_STEP = 3
F32 = jnp.float32
BF16 = jnp.bfloat16

X_TO = [['n', 'n', 'n', '', 'n', '', '', ''], ['nm', 'n', 'mn', 'n', '', 'n', 'p', 'p'], ['n', 'nm', 'n', 'n', 'mn', 'n', 'n', 'p'], ['n', 'n', 'n', 'n', '', '', 'n', '']]
S_MID = [[0, 0, 0, 0, 0, 0, 0], [1, 0, 0, 0, 0, 0, 0], [1, 1, 1, 1, 0, 0, 0], [0, 0, 0, 0, 0, 0, 0]]
IN_PREV = [[0, 1, 1, 1, 1, 1, 1, 1], [0, 1, 1, 1, 1, 1, 1, 1], [0, 0, 1, 1, 1, 1, 1, 1], [0, 0, 0, 0, 0, 1, 1, 1]]
IN_MID = [[0, 0, 0, 0, 0, 0, 0, 0], [0, 0, 0, 1, 1, 1, 1, 0], [0, 0, 0, 0, 0, 1, 0, 0], [0, 0, 0, 0, 0, 0, 0, 0]]
SERVE = [[0, 1, 3, 5, 7, 8, 10], [0, 1, 3, 5, 7, 5, 6], [0, 1, 3, 3, 2, 9, 3], [0, 1, 3, 5, 6, 7, 11]]


def chip_at(p):
    return jnp.where(p < RING // 2, p, 3 * RING // 2 - 1 - p)


def kernel(
    x_ref, wg_ref, wu_ref, wd_ref,
    y_ref, xg, tg, sg, hsave,
    w1, w2, xbuf, fbuf, gbuf, hbuf, sbuf,
    wsem, lsem, hsem, csem, xsend, xrecv, psend, precv, tsend, trecv, ssend, srecv,
):
    n = RING
    rows, dim = x_ref.shape
    half = rows // 2
    ff = wg_ref.shape[1]
    chunks = half // CHUNK

    me = lax.axis_index("tp")
    core = lax.rem(me, 2)
    pos = chip_at(me // 2)
    roles = (pos, n - 1 - pos)
    classes = tuple(lax.rem(q, 4) for q in roles)

    def device(p, c):
        return {"tp": chip_at(lax.rem(p + n, n)) * 2 + c}

    ahead = (device(pos + 1, core), device(pos - 1, core))
    behind = (ahead[1], ahead[0])
    across = device(n - 1 - pos, core)
    partner = device(pos, 1 - core)
    low = pl.ds(0, rows)
    high = pl.ds(rows, rows)

    def at(d, i):
        return pl.ds(pl.multiple_of(d * half + i * CHUNK, CHUNK), CHUNK)

    def any_class(d, flags):
        cond = None
        for c, flag in enumerate(flags):
            if flag:
                cond = (classes[d] == c) if cond is None else cond | (classes[d] == c)
        return cond

    def any_pair(d, s, table):
        cond = None
        for c, row in enumerate(table):
            for o, flag in enumerate(row):
                if flag:
                    hit = (classes[d] == c) & (s == o + 1)
                    cond = hit if cond is None else cond | hit
        return cond

    def across_at(d, o):
        return lax.rem(3 * n - 1 - 2 * roles[d] + o, n)

    def remote(src, dst, send, recv, to):
        return pltpu.make_async_remote_copy(
            src_ref=src, dst_ref=dst, send_sem=send, recv_sem=recv,
            device_id=to, device_id_type=pl.DeviceIdType.MESH,
        )

    def x_copy(o, d, i, kind):
        src = x_ref if o == 0 else xg.at[o, 0]
        slot = {"n": o + 1, "p": (o - 1) % n, "m": across_at(d, o)}[kind]
        to = {"n": ahead[d], "p": behind[d], "m": across}[kind]
        return remote(
            src.at[at(d, i)], xg.at[slot, 0, at(d, i)], xsend.at[o, "npm".index(kind), d, i], xrecv.at[slot, d, i], to
        )

    def x_arrived(o, d, i):
        return remote(xg.at[o, 0, at(d, i)], xg.at[o, 0, at(d, i)], xsend.at[o, 0, d, i], xrecv.at[o, d, i], ahead[d])

    def x_on(o, d, i, active, act):
        for kind in "npm":
            flags = [kind in X_TO[c][o] for c in range(4)]
            if not any(flags):
                continue
            cond = any_class(d, flags)

            @pl.when(cond if active is None else cond & active)
            def _():
                act(x_copy(o, d, i, kind))

    def x_side_own():
        return remote(x_ref, xg.at[0, 1], psend.at[0, 0, 0], precv.at[0, 0, 0], partner)

    def x_side(o, d, i):
        return remote(xg.at[o, 0, at(d, i)], xg.at[o, 1, at(d, i)], psend.at[o, d, i], precv.at[o, d, i], partner)

    def term_side(s, j):
        cols = pl.ds(pl.multiple_of(j * N2, N2), N2)
        return remote(xbuf.at[low, cols], tg.at[s, :, cols], tsend, trecv.at[s], partner)

    def term_all(s):
        return remote(xbuf.at[low], tg.at[s], tsend, trecv.at[s], partner)

    def out(s, d, i):
        return sbuf.at[lax.rem(s, 2), at(d, i)]

    def sum_copy(s, d, i, mid):
        if mid:
            slot = across_at(d, s)
            slot = jnp.where(slot == 0, n, slot)
            return remote(out(s, d, i), sg.at[slot, 1, at(d, i)], ssend.at[s, d, i], srecv.at[slot, 1, d, i], across)
        return remote(out(s, d, i), sg.at[s + 1, 0, at(d, i)], ssend.at[s, d, i], srecv.at[s + 1, 0, d, i], ahead[d])

    def sum_arrived(s, k, d, i):
        ref = sg.at[s, k, at(d, i)]
        return remote(ref, ref, ssend.at[s, d, i], srecv.at[s, k, d, i], ahead[d])

    def each(body):
        def go(i, c):
            body(i)
            return c

        lax.fori_loop(0, chunks, go, 0)

    tiles = 2 * ff // N1
    sub = N1 // 2

    def up_weights():
        out = []
        for j in range(tiles):
            src = pl.ds(j * sub, sub)
            out.append(pltpu.make_async_copy(wg_ref.at[:, src], w1.at[:, pl.ds(j * N1, sub)], wsem.at[2 * j]))
            out.append(pltpu.make_async_copy(wu_ref.at[:, src], w1.at[:, pl.ds(j * N1 + sub, sub)], wsem.at[2 * j + 1]))
        return out

    def down_weights():
        return pltpu.make_async_copy(wd_ref, w2, wsem.at[2 * tiles])

    def gate_up():
        def first(t, c):
            j, m = t // 2, lax.rem(t, 2)
            mine = pl.ds(pl.multiple_of(m * rows, rows), rows)
            cols = pl.ds(pl.multiple_of(j * N1, N1), N1)
            gbuf[...] = jnp.dot(xbuf[mine, :K1], w1[:K1, cols], preferred_element_type=F32)

            def deeper(k, c):
                ks = pl.ds(pl.multiple_of(k * K1, K1), K1)
                gbuf[...] += jnp.dot(xbuf[mine, ks], w1[ks, cols], preferred_element_type=F32)
                return c

            lax.fori_loop(1, dim // K1, deeper, 0)
            to = pl.ds(pl.multiple_of(j * sub, sub), sub)

            def gated(r, c):
                rs = pl.ds(pl.multiple_of(r * 32, 32), 32)
                ro = pl.ds(pl.multiple_of(m * rows + r * 32, 32), 32)
                hbuf[ro, to] = (jax.nn.silu(gbuf[rs, pl.ds(0, sub)]) * gbuf[rs, pl.ds(sub, sub)]).astype(BF16)
                return c

            return lax.fori_loop(0, rows // 32, gated, c)

        lax.fori_loop(0, 2 * tiles, first, 0)

    def project(s, between):
        def second(j, c):
            cols = pl.ds(pl.multiple_of(j * N2, N2), N2)
            term = jnp.dot(hbuf[...], w2[:, cols], preferred_element_type=F32)
            fbuf[:, cols] = term[:rows]
            xbuf[low, cols] = term[rows:].astype(BF16)
            term_side(s, j).start()
            return c

        lax.fori_loop(0, dim // N2, second, 0)
        between()
        term_all(s).wait_send()

    def serve(point):
        for o in range(1, n):
            for d in range(2):
                active = None
                for c in range(4):
                    hit = (classes[d] == c) & (point == SERVE[c][o - 1])
                    active = hit if active is None else active | hit

                @pl.when(active)
                def _():
                    def body(i):
                        x_arrived(o, d, i).wait_recv()
                        x_on(o, d, i, None, lambda copy: copy.start())
                        x_side(o, d, i).start()

                    each(body)

    def own_load(s):
        return pltpu.make_async_copy(xg.at[s, 0], xbuf.at[low], lsem.at[0])

    def load_x(s):
        own_load(s).start()

        def body(i):
            for d in range(2):
                x_side(s, d, i).wait_recv()

        each(body)
        side = pltpu.make_async_copy(xg.at[s, 1], xbuf.at[high], lsem.at[1])
        side.start()
        own_load(s).wait()
        side.wait()

    def term_load(s):
        return pltpu.make_async_copy(tg.at[s], xbuf.at[high], lsem.at[0])

    def add_on(s):
        comes = [(any_pair(d, s, IN_PREV), any_pair(d, s, IN_MID)) for d in range(2)]
        crosses = [any_pair(d, s, S_MID) for d in range(2)]

        def fold(j, c):
            cols = pl.ds(pl.multiple_of(j * N2, N2), N2)
            fbuf[:, cols] += xbuf[high, cols].astype(F32)
            return c

        term_load(s).wait()
        lax.fori_loop(0, dim // N2, fold, 0)

        def under(d, i):
            return pl.ds(pl.multiple_of(rows + d * half + i * CHUNK, CHUNK), CHUNK)

        def body(i):
            def staged(d):
                return (
                    pltpu.make_async_copy(sg.at[s, 0, at(d, i)], xbuf.at[at(d, i)], csem.at[d, 0]),
                    pltpu.make_async_copy(sg.at[s, 1, at(d, i)], xbuf.at[under(d, i)], csem.at[d, 1]),
                )

            for d in range(2):
                @pl.when(comes[d][1])
                def _():
                    sum_arrived(s, 1, d, i).wait_recv()
                    staged(d)[1].start()

                @pl.when(comes[d][0])
                def _():
                    sum_arrived(s, 0, d, i).wait_recv()
                    staged(d)[0].start()

            for d in range(2):
                @pl.when(s > 2)
                def _():
                    sum_copy(s - 2, d, i, False).wait_send()

                @pl.when(comes[d][1])
                def _():
                    staged(d)[1].wait()
                    fbuf[at(d, i), :] += xbuf[under(d, i), :].astype(F32)

                @pl.when(comes[d][0])
                def _():
                    staged(d)[0].wait()
                    out(s, d, i)[...] = (fbuf[at(d, i), :] + xbuf[at(d, i), :].astype(F32)).astype(BF16)

                @pl.when(jnp.logical_not(comes[d][0]))
                def _():
                    out(s, d, i)[...] = fbuf[at(d, i), :].astype(BF16)

                @pl.when((s < n) & crosses[d])
                def _():
                    sum_copy(s, d, i, True).start()

                @pl.when((s < n) & jnp.logical_not(crosses[d]))
                def _():
                    sum_copy(s, d, i, False).start()

                @pl.when(s == n)
                def _():
                    y_copy(d, i).start()

        each(body)

    def y_copy(d, i):
        return pltpu.make_async_copy(out(n, d, i), y_ref.at[at(d, i)], ssend.at[n, d, i])

    barrier = pltpu.get_barrier_semaphore()
    for other in (*ahead, across, partner):
        pl.semaphore_signal(barrier, inc=1, device_id=other, device_id_type=pl.DeviceIdType.MESH)
    pl.semaphore_wait(barrier, 4)

    def send_first(i):
        for d in range(2):
            x_on(0, d, i, None, lambda copy: copy.start())

    each(send_first)
    x_side_own().start()
    for copy in up_weights():
        copy.start()
    down_weights().start()
    serve(0)
    load_x(1)
    for copy in up_weights():
        copy.wait()
    gate_up()
    down_weights().wait()

    def saved(to_hbm):
        if to_hbm:
            return pltpu.make_async_copy(hbuf, hsave, hsem)
        return pltpu.make_async_copy(hsave, hbuf, hsem)

    def step(s, carry):
        @pl.when((s > 0) & (s < n - 1))
        def _():
            load_x(s + 1)
            gate_up()

        @pl.when(s == n - 1)
        def _():
            saved(False).start()
            saved(False).wait()

        @pl.when(s > 0)
        def _():
            term_all(s).wait_recv()
            term_load(s).start()
            serve(2 * s)
            add_on(s)

        @pl.when(s < n)
        def _():
            project(s + 1, lambda: serve(2 * s + 1))

        @pl.when(s == OWN_STEP)
        def _():
            own = pltpu.make_async_copy(x_ref, xbuf.at[low], lsem.at[0])
            own.start()
            x_side_own().wait_recv()
            side = pltpu.make_async_copy(xg.at[0, 1], xbuf.at[high], lsem.at[1])
            side.start()
            own.wait()
            side.wait()
            gate_up()
            saved(True).start()
            saved(True).wait()

        return carry

    lax.fori_loop(0, n + 1, step, 0)

    def finish(i):
        for d in range(2):
            for o in range(n):
                x_on(o, d, i, None, lambda copy: copy.wait_send())
                if o:
                    x_side(o, d, i).wait_send()
            sum_copy(n - 1, d, i, False).wait_send()
            y_copy(d, i).wait()

    each(finish)
    x_side_own().wait_send()


def solution(mesh):
    assert mesh.shape["tp"] == 2 * RING

    def step(x, w_gate, w_up, w_down):
        rows, dim = x.shape
        ff = w_gate.shape[1]
        n = RING
        chunks = rows // 2 // CHUNK
        hbm = pl.BlockSpec(memory_space=pl.ANY)
        dma = pltpu.SemaphoreType.DMA
        outs = pl.pallas_call(
            kernel,
            out_shape=[
                jax.ShapeDtypeStruct((rows, dim), BF16),
                jax.ShapeDtypeStruct((n, 2, rows, dim), BF16),
                jax.ShapeDtypeStruct((n + 1, rows, dim), BF16),
                jax.ShapeDtypeStruct((n + 1, 2, rows, dim), BF16),
                jax.ShapeDtypeStruct((2 * rows, ff), BF16),
            ],
            in_specs=[hbm] * 4,
            out_specs=[hbm] * 5,
            scratch_shapes=[
                pltpu.VMEM((dim, 2 * ff), BF16),
                pltpu.VMEM((ff, dim), BF16),
                pltpu.VMEM((2 * rows, dim), BF16),
                pltpu.VMEM((rows, dim), F32),
                pltpu.VMEM((rows, N1), F32),
                pltpu.VMEM((2 * rows, ff), BF16),
                pltpu.VMEM((2, rows, dim), BF16),
                dma((4 * ff // N1 + 1,)),
                dma((2,)),
                dma,
                dma((2, 2)),
                dma((n, 3, 2, chunks)),
                dma((n, 2, chunks)),
                dma((n, 2, chunks)),
                dma((n, 2, chunks)),
                dma,
                dma((n + 1,)),
                dma((n + 1, 2, chunks)),
                dma((n + 1, 2, 2, chunks)),
            ],
            compiler_params=pltpu.CompilerParams(
                collective_id=0, has_side_effects=True, vmem_limit_bytes=67043328
            ),
        )(x, w_gate, w_up, w_down)
        return outs[0]

    return jax.shard_map(
        step,
        mesh=mesh,
        in_specs=(P(("dp", "tp"), None), P(None, "tp"), P(None, "tp"), P("tp", None)),
        out_specs=P(("dp", "tp"), None),
        check_vma=False,
    )
```

time: 724 us -> 341 us (0.47)
  waiting for transfers between devices: 542 us -> 0 us
  Pallas kernels: 0 us -> 336 us
  matrix products: 169 us -> 0 us
  between operations: 13.4 us -> 0.01 us
    reduce_scatter x1 -> x0, waiting for transfers between devices: 354 us -> none  [step(): return lax.psum_scatter(term, 'tp', scatter_dimension=0, tiled=True)]
    pallas_call x0 -> x1, Pallas kernels: none -> 336 us  [step(): pl.pallas_call(kernel, out_shape=[jax.ShapeDtypeStruct((rows, dim), BF16)...]
    all_gather x1 -> x0, waiting for transfers between devices: 187 us -> none  [step(): rows = lax.all_gather(x, 'tp', axis=0, tiled=True)]
    dot_general x3 -> x0, matrix products: 169 us -> none  [the longest x1 57.3 us: step(): gate = jnp.dot(rows, w_gate, preferred_element_type=jnp.float32)]
  transfers between devices with their start and end apart: 2 -> 0, of which waited for: 2 -> 0; matrix products, arithmetic and copies ran while one was open for 0% -> 0% of each run, Pallas kernels for 0% -> 0%
where the time goes in v2:
time: 341 us; the launch traced here: 340 us
  Pallas kernels  336 us (99%)
    pallas_call x1, Pallas kernels, step(): pl.pallas_call(kernel, out_shape=[jax.ShapeDtypeStruct((rows, dim), BF16)...  336 us

profile of v2, /device:TPU:0, one launch (start us, length us, event | category | flops | bytes accessed | tf_op | source)
XLA Modules:
  0.0 339.6 jit_solution(10109184778712810012)
XLA Ops:
  0.0 336.4 %shard_map.46 = (bf16[160,7168]{1,0:T(8,128)(2,1)}, bf16[8,2,160,7168]{3,2,1,0:T(8,128)(2,1)}, bf16[9,160,7168]{2,1,0:T(8,128)(2,1)}, bf16[9,2,160,7168]{3,2,1,0:T(8,128)(2,1)}, bf16[320,1152]{1,0:T(8,128)(2,1)}) custom-call(bf16[160,7168]{1,0:T(8,128)(2,1)} %x_ref.1, bf16[7168,1152]{1,0:T(8,128)(2,1)} %wg_ref.1, bf16[7168,1152]{1,0:T(8,128)(2,1)} %wu_ref.1, ...), custom_call_target="tpu_custom_call" | custom-call | tf_op jit(solution)/shard_map/pallas_call | solution.py:385
  336.5 3.2 copy.6

commit v3 on v2

--- a/solution.py
+++ b/solution.py
@@ -15,10 +15,10 @@
 BF16 = jnp.bfloat16
 
 X_TO = [['n', 'n', 'n', '', 'n', '', '', ''], ['nm', 'n', 'mn', 'n', '', 'n', 'p', 'p'], ['n', 'nm', 'n', 'n', 'mn', 'n', 'n', 'p'], ['n', 'n', 'n', 'n', '', '', 'n', '']]
-S_MID = [[0, 0, 0, 0, 0, 0, 0], [1, 0, 0, 0, 0, 0, 0], [1, 1, 1, 1, 0, 0, 0], [0, 0, 0, 0, 0, 0, 0]]
-IN_PREV = [[0, 1, 1, 1, 1, 1, 1, 1], [0, 1, 1, 1, 1, 1, 1, 1], [0, 0, 1, 1, 1, 1, 1, 1], [0, 0, 0, 0, 0, 1, 1, 1]]
-IN_MID = [[0, 0, 0, 0, 0, 0, 0, 0], [0, 0, 0, 1, 1, 1, 1, 0], [0, 0, 0, 0, 0, 1, 0, 0], [0, 0, 0, 0, 0, 0, 0, 0]]
-SERVE = [[0, 1, 3, 5, 7, 8, 10], [0, 1, 3, 5, 7, 5, 6], [0, 1, 3, 3, 2, 9, 3], [0, 1, 3, 5, 6, 7, 11]]
+S_MID = [[0, 0, 0, 0, 0, 0, 0], [1, 1, 0, 0, 0, 0, 0], [1, 1, 1, 1, 1, 0, 0], [0, 0, 0, 0, 0, 0, 0]]
+IN_PREV = [[0, 1, 1, 1, 1, 1, 1, 1], [0, 1, 1, 1, 1, 1, 1, 1], [0, 0, 0, 1, 1, 1, 1, 1], [0, 0, 0, 0, 0, 0, 1, 1]]
+IN_MID = [[0, 0, 0, 0, 0, 0, 0, 0], [0, 0, 0, 1, 1, 1, 1, 1], [0, 0, 0, 0, 0, 1, 1, 0], [0, 0, 0, 0, 0, 0, 0, 0]]
+SERVE = [[2, 3, 7, 12, 16, 20, 24], [2, 3, 7, 6, 16, 13, 15], [2, 3, 8, 10, 3, 20, 7], [2, 3, 8, 12, 15, 15, 24]]
 
 
 def chip_at(p):
@@ -151,9 +151,11 @@
     def down_weights():
         return pltpu.make_async_copy(wd_ref, w2, wsem.at[2 * tiles])
 
-    def gate_up():
+    def gate_up(late=None, halfway=None):
         def first(t, c):
-            j, m = t // 2, lax.rem(t, 2)
+            j, m = lax.rem(t, tiles), t // tiles
+            if late is not None:
+                pl.when(t == tiles)(lambda: side_load(late).wait())
             mine = pl.ds(pl.multiple_of(m * rows, rows), rows)
             cols = pl.ds(pl.multiple_of(j * N1, N1), N1)
             gbuf[...] = jnp.dot(xbuf[mine, :K1], w1[:K1, cols], preferred_element_type=F32)
@@ -172,7 +174,12 @@
                 hbuf[ro, to] = (jax.nn.silu(gbuf[rs, pl.ds(0, sub)]) * gbuf[rs, pl.ds(sub, sub)]).astype(BF16)
                 return c
 
-            return lax.fori_loop(0, rows // 32, gated, c)
+            lax.fori_loop(0, rows // 32, gated, 0)
+            if late is not None:
+                pl.when(t == 0)(lambda: side_start(late))
+            if halfway is not None:
+                pl.when(t == tiles - 1)(halfway)
+            return c
 
         lax.fori_loop(0, 2 * tiles, first, 0)
 
@@ -209,18 +216,20 @@
     def own_load(s):
         return pltpu.make_async_copy(xg.at[s, 0], xbuf.at[low], lsem.at[0])
 
-    def load_x(s):
-        own_load(s).start()
-
+    def side_load(s):
+        return pltpu.make_async_copy(xg.at[s, 1], xbuf.at[high], lsem.at[1])
+
+    def side_start(s):
         def body(i):
             for d in range(2):
                 x_side(s, d, i).wait_recv()
 
         each(body)
-        side = pltpu.make_async_copy(xg.at[s, 1], xbuf.at[high], lsem.at[1])
-        side.start()
+        side_load(s).start()
+
+    def load_x(s):
+        own_load(s).start()
         own_load(s).wait()
-        side.wait()
 
     def term_load(s):
         return pltpu.make_async_copy(tg.at[s], xbuf.at[high], lsem.at[0])
@@ -308,11 +317,11 @@
     for copy in up_weights():
         copy.start()
     down_weights().start()
-    serve(0)
+    serve(2)
     load_x(1)
     for copy in up_weights():
         copy.wait()
-    gate_up()
+    gate_up(1)
     down_weights().wait()
 
     def saved(to_hbm):
@@ -323,8 +332,9 @@
     def step(s, carry):
         @pl.when((s > 0) & (s < n - 1))
         def _():
+            serve(4 * s)
             load_x(s + 1)
-            gate_up()
+            gate_up(s + 1, lambda: serve(4 * s + 1))
 
         @pl.when(s == n - 1)
         def _():
@@ -335,12 +345,12 @@
         def _():
             term_all(s).wait_recv()
             term_load(s).start()
-            serve(2 * s)
+            serve(4 * s + 2)
             add_on(s)
 
         @pl.when(s < n)
         def _():
-            project(s + 1, lambda: serve(2 * s + 1))
+            project(s + 1, lambda: serve(4 * s + 3))
 
         @pl.when(s == OWN_STEP)
         def _():

time: 341 us -> 324 us (0.950)
  Pallas kernels: 336 us -> 319 us
    pallas_call x1, Pallas kernels: 336 us -> 319 us  [step(): pl.pallas_call(kernel, out_shape=[jax.ShapeDtypeStruct((rows, dim), BF16)...]
where the time goes in v3:
time: 324 us; the launch traced here: 322 us
  Pallas kernels  319 us (98%)
    pallas_call x1, Pallas kernels, step(): pl.pallas_call(kernel, out_shape=[jax.ShapeDtypeStruct((rows, dim), BF16)...  319 us

profile of v3, /device:TPU:0, one launch (start us, length us, event | category | flops | bytes accessed | tf_op | source)
XLA Modules:
  0.0 321.9 jit_solution(11417886298994761596)
XLA Ops:
  0.0 318.7 %shard_map.46 = (bf16[160,7168]{1,0:T(8,128)(2,1)}, bf16[8,2,160,7168]{3,2,1,0:T(8,128)(2,1)}, bf16[9,160,7168]{2,1,0:T(8,128)(2,1)}, bf16[9,2,160,7168]{3,2,1,0:T(8,128)(2,1)}, bf16[320,1152]{1,0:T(8,128)(2,1)}) custom-call(bf16[160,7168]{1,0:T(8,128)(2,1)} %x_ref.1, bf16[7168,1152]{1,0:T(8,128)(2,1)} %wg_ref.1, bf16[7168,1152]{1,0:T(8,128)(2,1)} %wu_ref.1, ...), custom_call_target="tpu_custom_call" | custom-call | tf_op jit(solution)/shard_map/pallas_call | solution.py:395
  318.7 3.2 copy.6
